TPU v7x, 32 devices: a whole 2x2x4 slice. The times are simulated.
32 devices in a mesh: pa: 16 (over z, y, core), pb: 2 (over x).
Axes of the slice: x: 2, y: 2, z: 4, core: 2. Of those that a mesh axis runs over, the one named last changes fastest.
Arguments:
- sources: float32 [4096, 128], P(('pa', 'pb')), may hold values from -3 to 3, as said below
- targets: bfloat16 [4096, 128], P(('pa', 'pb')), may hold values from -2 to 2, as said below
- source_mass: float32 [4096], P(('pa', 'pb')), may hold values from -1 to 1
- target_mass: float32 [4096], P(('pa', 'pb')), may hold values from -1 to 1
Outputs:
- moved: float32 [4096, 128], P(('pa', 'pb'))
- dual_source: float32 [4096], P(('pa', 'pb'))
- dual_target: float32 [4096], P(('pa', 'pb'))
Inputs may be any that keep to these rules, and one draw needn't show every extreme that they name: `targets`: each block of 128 target rows is drawn around one cluster centre, a different one for each block. `sources`: each block of 128 source rows is drawn around a cluster centre of its own, drawn independently of the target centres, possibly offset by a common shift.
All inputs are finite; a program needn't handle non-finite values.
Results may differ from a plain program's by a relative error of at most 0.003.
Values may be sent and summed in bfloat16 or wider, within the bound.
A program may use at most 64 MiB of HBM per device.

v0:
```python
from functools import partial
import jax
import jax.numpy as jnp
from jax import lax
from jax.sharding import PartitionSpec as P

STEPS = 1
ITERS = 2
step_rate = 0.25
floor_value = -1e30


def merged(part, axis, combine):
    gathered = jax.tree.map(lambda a: lax.all_gather(a, axis), part)

    def take(source):
        return jax.tree.map(lambda a: lax.dynamic_index_in_dim(a, source, 0, False), gathered)

    return lax.fori_loop(
        1, lax.axis_size(axis), lambda source, state: combine(state, take(source)), take(0)
    )


def squares(coords):
    wide = coords.astype(jnp.float32)
    return jnp.sum(wide * wide, axis=1)


def pair_cost(left, left_norm, right, right_norm):
    inner = lax.dot_general(
        left, right, (((1,), (1,)), ((), ())), preferred_element_type=jnp.float32
    )
    return left_norm[:, None] + right_norm[None, :] - 2.0 * inner


def over_blocks(update, carry, total):
    block_width = 512 if total % 512 == 0 else total
    block_count = total // block_width
    if block_count == 1:
        return update(carry, 0, block_width)
    return lax.fori_loop(
        0,
        block_count,
        lambda position, current: update(current, position * block_width, block_width),
        carry,
    )


def lse_piece(rows, row_norm, columns, column_norm, carry, piece, start):

    def update(current, offset, length):
        chosen = lax.dynamic_slice_in_dim(columns, start + offset, length, 0)
        chosen_norm = lax.dynamic_slice_in_dim(column_norm, start + offset, length, 0)
        values = lax.dynamic_slice_in_dim(piece, offset, length, 0)
        scores = values[None, :] - pair_cost(rows, row_norm, chosen, chosen_norm)
        highest, totals = current
        raised = jnp.maximum(highest, jnp.max(scores, axis=1))
        totals = totals * jnp.exp(highest - raised) + jnp.sum(
            jnp.exp(scores - raised[:, None]), axis=1
        )
        return (raised, totals)

    return over_blocks(update, carry, piece.shape[0])


def plan_piece(rows, row_norm, row_pot, columns, column_norm, carry, piece, start):

    def update(current, offset, length):
        chosen = lax.dynamic_slice_in_dim(columns, start + offset, length, 0)
        chosen_norm = lax.dynamic_slice_in_dim(column_norm, start + offset, length, 0)
        values = lax.dynamic_slice_in_dim(piece, offset, length, 0)
        cost = pair_cost(rows, row_norm, chosen, chosen_norm)
        weights = jnp.exp(row_pot[:, None] + values[None, :] - cost).astype(jnp.bfloat16)
        return current + jnp.dot(weights, chosen, preferred_element_type=jnp.float32)

    return over_blocks(update, carry, piece.shape[0])


def join_lse(first, second):
    raised = jnp.maximum(first[0], second[0])
    return (raised, first[1] * jnp.exp(first[0] - raised) + second[1] * jnp.exp(second[0] - raised))


def start_lse(length):
    return (jnp.full((length,), floor_value, jnp.float32), jnp.zeros((length,), jnp.float32))


def finish(carry):
    return -(carry[0] + jnp.log(carry[1]))


def body(sources, targets, source_mass, target_mass):
    own_rows = sources.shape[0]
    own_targets = targets.shape[0]
    target_norm = squares(targets)
    moving = sources
    dual_target = jnp.zeros((own_targets,), jnp.float32)
    dual_source = jnp.zeros((own_rows,), jnp.float32)
    member = lax.axis_index("pb")
    half_targets = lax.all_gather(targets, "pa", axis=0, tiled=True)
    half_norm = squares(half_targets)
    pair_mass = lax.all_gather(source_mass, "pb", axis=0, tiled=True)
    pair_dual = jnp.zeros((pair_mass.shape[0],), jnp.float32)
    for flow_step in range(STEPS):
        coarse = moving.astype(jnp.bfloat16)
        pair_coarse = lax.all_gather(coarse, "pb", axis=0, tiled=True)
        pair_norm = squares(pair_coarse)
        pair_count = pair_coarse.shape[0]
        all_sources = lax.all_gather(pair_coarse, "pa", axis=0, tiled=True)
        all_source_norm = squares(all_sources)
        row_fold = partial(lse_piece, pair_coarse, pair_norm, half_targets, half_norm)
        column_fold = partial(lse_piece, targets, target_norm, all_sources, all_source_norm)
        shifted = dual_target + target_mass
        for sweep in range(ITERS + 1):
            shifted = dual_target + target_mass
            half_lse = row_fold(
                start_lse(pair_count),
                jax.tree.map(lambda part: lax.all_gather(part, "pa", axis=0, tiled=True), shifted),
                jnp.int32(0),
            )
            pair_dual = finish(merged((half_lse[0], half_lse[1]), "pb", join_lse))
            if sweep < ITERS:
                lifted = pair_dual + pair_mass
                dual_target = finish(
                    column_fold(
                        start_lse(own_targets),
                        jax.tree.map(
                            lambda part: lax.all_gather(part, "pa", axis=0, tiled=True), lifted
                        ),
                        jnp.int32(0),
                    )
                )
        plan_fold = partial(plan_piece, pair_coarse, pair_norm, pair_dual, half_targets, half_norm)
        empty = jnp.zeros((pair_count, sources.shape[1]), jnp.float32)
        pair_centre = plan_fold(
            empty,
            jax.tree.map(lambda part: lax.all_gather(part, "pa", axis=0, tiled=True), shifted),
            jnp.int32(0),
        )
        centre = lax.psum_scatter(
            pair_centre.astype(jnp.bfloat16), "pb", scatter_dimension=0, tiled=True
        ).astype(jnp.float32)
        moving = moving - 2.0 * step_rate * (moving - centre)
    dual_source = lax.dynamic_slice_in_dim(pair_dual, member * own_rows, own_rows, 0)
    return (moving, dual_source, dual_target)


def solution(mesh):
    return jax.shard_map(
        body,
        mesh=mesh,
        in_specs=(P(("pa", "pb"), None), P(("pa", "pb"), None), P(("pa", "pb")), P(("pa", "pb"))),
        out_specs=(P(("pa", "pb"), None), P(("pa", "pb")), P(("pa", "pb"))),
        check_vma=False,
    )
```

profile of v0, /device:TPU:0, one launch (start us, length us, event | category | flops | bytes accessed | tf_op | source)
XLA Modules:
  0.0 212.0 jit_solution(4313513718906820735)
XLA Ops:
  8.1 5.6 %all_gather.65 = bf16[256,128]{1,0:T(8,128)(2,1)} all-gather(bf16[128,128]{1,0:T(8,128)(2,1)S(1)} %convert_element_type.28), channel_id=1, replica_groups=mesh['pa'=16,'pb'=2] {'pb'}, dimensions={0}, use_global_device_ids=true | all-gather | bytes 98304 | tf_op jit(solution)/shard_map/all_gather | solution.py:106
  14.7 24.4 %all_gather.66 = bf16[2048,128]{1,0:T(8,128)(2,1)S(1)} all-gather(bf16[128,128]{1,0:T(8,128)(2,1)} %param.17), channel_id=1, replica_groups=mesh['pa'=16,'pb'=2] {'pa'}, dimensions={0}, use_global_device_ids=true | all-gather | bytes 557056 | tf_op jit(solution)/shard_map/all_gather | solution.py:100
  39.4 17.5 %all-gather.6 = f32[16,1,128]{2,1,0:T(1,128)S(1)} all-gather(f32[1,1,128]{2,1,0:T(1,128)S(1)} %bitcast.107), channel_id=1, replica_groups=mesh['pa'=16,'pb'=2] {'pa'}, dimensions={0}, use_global_device_ids=true | all-gather | bytes 8704 | tf_op jit(solution)/shard_map/all_gather | solution.py:118
  56.9 2.4 %while.112 = (s32[]{:T(128)}, f32[256]{0:T(256)S(1)}, f32[256]{0:T(256)S(1)}, f32[2048]{0:T(1024)S(1)}, f32[256]{0:T(256)S(1)}, /*index=5*/f32[2048]{0:T(1024)S(...) while((s32[]{:T(128)}, f32[256]{0:T(256)S(1)}, ...), condition=%wide.region_6.7_spmd.clone, body=%wide.region_3.6_spmd.clone.sunk | while | flops 34473220 | bytes 1271994 | solution.py:41
  59.4 4.2 %all-gather.9 = f32[2,1,128]{2,1,0:T(1,128)S(1)} all-gather(f32[1,1,128]{2,1,0:T(1,128)S(1)} %bitcast.124), channel_id=1, replica_groups=mesh['pa'=16,'pb'=2] {'pb'}, dimensions={0}, use_global_device_ids=true | all-gather | bytes 1536 | tf_op jit(solution)/shard_map/all_gather | solution.py:102
  63.7 4.2 %all-gather.7 = f32[2,1,256]{2,1,0:T(1,128)S(1)} all-gather(f32[1,1,256]{2,1,0:T(1,128)S(1)} %bitcast.98), channel_id=2, replica_groups=mesh['pa'=16,'pb'=2] {'pb'}, dimensions={0}, use_global_device_ids=true | all-gather | bytes 3072 | tf_op jit(solution)/shard_map/all_gather | solution.py:14
  67.9 4.2 %all-gather.8 = f32[2,1,256]{2,1,0:T(1,128)S(1)} all-gather(f32[1,1,256]{2,1,0:T(1,128)S(1)} %bitcast.106), channel_id=3, replica_groups=mesh['pa'=16,'pb'=2] {'pb'}, dimensions={0}, use_global_device_ids=true | all-gather | bytes 3072 | tf_op jit(solution)/shard_map/all_gather | solution.py:14
  72.2 18.8 %all-gather.10 = f32[16,1,256]{2,1,0:T(1,128)S(1)} all-gather(f32[1,1,256]{2,1,0:T(1,128)S(1)} %bitcast.113), channel_id=1, replica_groups=mesh['pa'=16,'pb'=2] {'pa'}, dimensions={0}, use_global_device_ids=true | all-gather | bytes 17408 | tf_op jit(solution)/shard_map/all_gather | solution.py:128
  91.2 1.8 multiply_reduce_fusion
  93.0 11.5 %while.113 = (s32[]{:T(128)}, f32[128]{0:T(128)S(1)}, f32[128]{0:T(128)S(1)}, f32[4096]{0:T(1024)S(1)}, f32[128]{0:T(128)S(1)}, /*index=5*/f32[4096]{0:T(1024)S(...) while((s32[]{:T(128)}, f32[128]{0:T(128)S(1)}, ...), condition=%wide.region_11.0_spmd.clone, body=%wide.region_8.11_spmd.clone.sunk | while | flops 17236612 | bytes 707770 | solution.py:41
  104.6 17.4 %all-gather.11 = f32[16,1,128]{2,1,0:T(1,128)S(1)} all-gather(f32[1,1,128]{2,1,0:T(1,128)S(1)} %add_bitcast_fusion.1), channel_id=1, replica_groups=mesh['pa'=16,'pb'=2] {'pa'}, dimensions={0}, use_global_device_ids=true | all-gather | bytes 8704 | tf_op jit(solution)/shard_map/all_gather | solution.py:118
  122.0 2.4 %while.114 = (s32[]{:T(128)}, f32[256]{0:T(256)S(1)}, f32[256]{0:T(256)S(1)}, f32[2048]{0:T(1024)S(1)}, f32[256]{0:T(256)S(1)}, /*index=5*/f32[2048]{0:T(1024)S(...) while((s32[]{:T(128)}, f32[256]{0:T(256)S(1)}, ...), condition=%wide.region_15.0_spmd.clone, body=%wide.region_12.15_spmd.clone.sunk | while | flops 34473220 | bytes 1271994 | solution.py:41
  124.4 4.2 %all-gather.12 = f32[2,1,256]{2,1,0:T(1,128)S(1)} all-gather(f32[1,1,256]{2,1,0:T(1,128)S(1)} %bitcast.97), channel_id=4, replica_groups=mesh['pa'=16,'pb'=2] {'pb'}, dimensions={0}, use_global_device_ids=true | all-gather | bytes 3072 | tf_op jit(solution)/shard_map/all_gather | solution.py:14
  128.7 4.2 %all-gather.13 = f32[2,1,256]{2,1,0:T(1,128)S(1)} all-gather(f32[1,1,256]{2,1,0:T(1,128)S(1)} %bitcast.105), channel_id=5, replica_groups=mesh['pa'=16,'pb'=2] {'pb'}, dimensions={0}, use_global_device_ids=true | all-gather | bytes 3072 | tf_op jit(solution)/shard_map/all_gather | solution.py:14
  132.9 18.8 %all-gather.14 = f32[16,1,256]{2,1,0:T(1,128)S(1)} all-gather(f32[1,1,256]{2,1,0:T(1,128)S(1)} %bitcast.112), channel_id=1, replica_groups=mesh['pa'=16,'pb'=2] {'pa'}, dimensions={0}, use_global_device_ids=true | all-gather | bytes 17408 | tf_op jit(solution)/shard_map/all_gather | solution.py:128
  151.7 11.5 %while.115 = (s32[]{:T(128)}, f32[128]{0:T(128)S(1)}, f32[128]{0:T(128)S(1)}, f32[4096]{0:T(1024)S(1)}, f32[128]{0:T(128)S(1)}, /*index=5*/f32[4096]{0:T(1024)S(...) while((s32[]{:T(128)}, f32[128]{0:T(128)S(1)}, ...), condition=%wide.region_19.20_spmd.clone, body=%wide.region_16.19_spmd.clone.sunk | while | flops 17236612 | bytes 707770 | solution.py:41
  160.5 1.1 fusion.116
  163.8 17.4 %all-gather.15 = f32[16,1,128]{2,1,0:T(1,128)S(1)} all-gather(f32[1,1,128]{2,1,0:T(1,128)S(1)} %get-tuple-element.1165), channel_id=1, replica_groups=mesh['pa'=16,'pb'=2] {'pa'}, dimensions={0}, use_global_device_ids=true | all-gather | bytes 8704 | tf_op jit(solution)/shard_map/all_gather | solution.py:137
  181.2 2.4 %while.116 = (s32[]{:T(128)}, f32[256]{0:T(256)S(1)}, f32[256]{0:T(256)S(1)}, f32[2048]{0:T(1024)S(1)}, f32[256]{0:T(256)S(1)}, /*index=5*/f32[2048]{0:T(1024)S(...) while((s32[]{:T(128)}, f32[256]{0:T(256)S(1)}, ...), condition=%wide.region_23.24_spmd.clone, body=%wide.region_20.23_spmd.clone.sunk | while | flops 34473220 | bytes 1271994 | solution.py:41
  183.6 4.2 %all-gather.16 = f32[2,1,256]{2,1,0:T(1,128)S(1)} all-gather(f32[1,1,256]{2,1,0:T(1,128)S(1)} %bitcast.96), channel_id=6, replica_groups=mesh['pa'=16,'pb'=2] {'pb'}, dimensions={0}, use_global_device_ids=true | all-gather | bytes 3072 | tf_op jit(solution)/shard_map/all_gather | solution.py:14
  187.9 4.2 %all-gather.17 = f32[2,1,256]{2,1,0:T(1,128)S(1)} all-gather(f32[1,1,256]{2,1,0:T(1,128)S(1)} %bitcast.104), channel_id=7, replica_groups=mesh['pa'=16,'pb'=2] {'pb'}, dimensions={0}, use_global_device_ids=true | all-gather | bytes 3072 | tf_op jit(solution)/shard_map/all_gather | solution.py:14
  192.1 2.4 %while.117 = (s32[]{:T(128)}, f32[256,128]{1,0:T(8,128)S(1)}, f32[256]{0:T(256)S(1)}, f32[2048]{0:T(1024)S(1)}, f32[256]{0:T(256)S(1)}, /*index=5*/f32[2048]{0:T...) while((s32[]{:T(128)}, f32[256,128]{1,0:T(8,128)S(1)}, ...), condition=%wide.region_25.0_spmd.clone, body=%wide.region_24.25_spmd.clone.sunk | while | flops 67960840 | bytes 605876 | solution.py:41
  195.8 8.0 %reduce-scatter.2.cloned.1.call-done = bf16[128,128]{1,0:T(8,128)(2,1)} async-done(((bf16[256,128]{1,0:T(8,128)(2,1)}), bf16[128,128]{1,0:T(8,128)(2,1)}) %reduce-scatter.2.cloned.1.call-update) | async-done | bytes 32784 | tf_op jit(solution)/shard_map/reduce_scatter | solution.py:140
  203.7 1.4 multiply_subtract_fusion
  (250 shorter events, 34.7 us)
Async XLA Ops:
  7.2 32.3 %copy-start.3 = (f32[128]{0:T(128)S(1)}, f32[128]{0:T(128)}, u32[]{:S(2)}) copy-start(f32[128]{0:T(128)} %param.19) | copy-start | bytes 1540
  7.2 84.0 %all-gather.20.cloned.1.call-start = ((), (), s32[]{:S(2)}) async-start(), calls=%async_computation.1 | async-start | bytes 1114112 | tf_op jit(solution)/shard_map/all_gather | solution.py:109
  13.7 43.2 %copy-start = (bf16[256,128]{1,0:T(8,128)(2,1)S(1)}, bf16[256,128]{1,0:T(8,128)(2,1)}, u32[]{:S(2)}) copy-start(bf16[256,128]{1,0:T(8,128)(2,1)} %all_gather.65) | copy-start | bytes 196612
  13.7 190.0 %reduce-scatter.2.cloned.1.call-start = ((), (), s32[]{:S(2)}) async-start(), calls=%async_computation.2 | async-start | bytes 98304 | tf_op jit(solution)/shard_map/reduce_scatter | solution.py:140
  56.9 2.5 %copy-start.4 = (f32[128]{0:T(128)S(1)}, f32[128]{0:T(128)}, u32[]{:S(2)}) copy-start(f32[128]{0:T(128)} %param.18) | copy-start | bytes 1540
  56.9 34.1 %copy-start.2 = (bf16[128,128]{1,0:T(8,128)(2,1)S(1)}, bf16[128,128]{1,0:T(8,128)(2,1)}, u32[]{:S(2)}) copy-start(bf16[128,128]{1,0:T(8,128)(2,1)} %param.17) | copy-start | bytes 98308
  192.1 11.6 %copy-start.1 = (f32[128,128]{1,0:T(8,128)S(1)}, f32[128,128]{1,0:T(8,128)}, u32[]{:S(2)}) copy-start(f32[128,128]{1,0:T(8,128)} %param.16) | copy-start | bytes 196612
Sparse Core Ops, SparseCore 0:
  13.8 40.4 all-gather.19
  195.3 8.3 reduce-scatter.1
where the time goes:
time: 213 us; the launch traced here: 212 us
  blocking collectives  150 us (70%)
  matrix products  23.1 us (11%)
  between operations  14.3 us (7%)
  other arithmetic  10.3 us (5%)
  waiting for transfers between devices  8.02 us (4%)
  local copies, waits for them, and re-layouts  5.52 us (3%)
    all_gather x5, blocking collectives, body(): lax.all_gather(part, 'pa', axis=0, tiled=True)  90 us
    all_gather x6, blocking collectives, merged(): gathered = jax.tree.map(lambda a: lax.all_gather(a, axis), part)  25.4 us
    all_gather x1, blocking collectives, body(): half_targets = lax.all_gather(targets, 'pa', axis=0, tiled=True)  24.4 us
    dot_general x28, matrix products, pair_cost(): lax.dot_general(left, right, (((1,), (1,)), ((), ())), preferred_element_...  21.5 us
    reduce_scatter x1, waiting for transfers between devices, body(): lax.psum_scatter(pair_centre.astype(jnp.bfloat16), 'pb', scatter_dimensio...  7.97 us
    all_gather x1, blocking collectives, body(): pair_coarse = lax.all_gather(coarse, 'pb', axis=0, tiled=True)  5.6 us
  transfers between devices with their start and end apart: 2, of which 1 were waited for; matrix products, arithmetic and copies ran while one was open for 2% of the time, Pallas kernels for 0%

commit v1 on v0

--- a/solution.py
+++ b/solution.py
@@ -97,7 +97,14 @@
     dual_target = jnp.zeros((own_targets,), jnp.float32)
     dual_source = jnp.zeros((own_rows,), jnp.float32)
     member = lax.axis_index("pb")
-    half_targets = lax.all_gather(targets, "pa", axis=0, tiled=True)
+    parts_seen = [targets]
+    nodes = jax.lax.psum(1, "pa")
+    for num in range(nodes - 1):
+        front = jax.lax.ppermute(parts_seen[-1], "pa", [(q, (q + 1) % nodes) for q in range(nodes)])
+        parts_seen.append(front)
+    upper = jnp.concatenate(parts_seen[::-1], axis=0)
+    mid_arr = jax.lax.axis_index("pa")
+    half_targets = jnp.roll(upper, shift=(mid_arr + 1) * targets.shape[0], axis=0)
     half_norm = squares(half_targets)
     pair_mass = lax.all_gather(source_mass, "pb", axis=0, tiled=True)
     pair_dual = jnp.zeros((pair_mass.shape[0],), jnp.float32)

time: 213 us -> 269 us (1.26)
  waiting for transfers between devices: 8.02 us -> 87.1 us
  blocking collectives: 150 us -> 125 us
    ppermute x0 -> x15, waiting for transfers between devices: none -> 78.7 us  [body(): jax.lax.ppermute(parts_seen[-1], 'pa', [(q, (q + 1) % nodes) for q in ran...]
    all_gather x1 -> x0, blocking collectives: 24.4 us -> none  [body(): half_targets = lax.all_gather(targets, 'pa', axis=0, tiled=True)]
  transfers between devices with their start and end apart: 2 -> 17, of which waited for: 1 -> 15; matrix products, arithmetic and copies ran while one was open for 2% -> 2% of each run, Pallas kernels for 0% -> 0%
where the time goes in v1:
time: 269 us; the launch traced here: 268 us
  blocking collectives  125 us (46%)
  waiting for transfers between devices  87.1 us (32%)
  matrix products  23.2 us (9%)
  between operations  14.5 us (5%)
  other arithmetic  11.1 us (4%)
  local copies, waits for them, and re-layouts  6.07 us (2%)
    all_gather x5, blocking collectives, body(): lax.all_gather(part, 'pa', axis=0, tiled=True)  90.1 us
    ppermute x15, waiting for transfers between devices, body(): jax.lax.ppermute(parts_seen[-1], 'pa', [(q, (q + 1) % nodes) for q in ran...  78.7 us
    all_gather x6, blocking collectives, merged(): gathered = jax.tree.map(lambda a: lax.all_gather(a, axis), part)  25.4 us
    dot_general x28, matrix products, pair_cost(): lax.dot_general(left, right, (((1,), (1,)), ((), ())), preferred_element_...  21.5 us
    reduce_scatter x1, waiting for transfers between devices, body(): lax.psum_scatter(pair_centre.astype(jnp.bfloat16), 'pb', scatter_dimensio...  8.39 us
  transfers between devices with their start and end apart: 17, of which 15 were waited for; matrix products, arithmetic and copies ran while one was open for 2% of the time, Pallas kernels for 0%

profile of v1, /device:TPU:0, one launch (start us, length us, event | category | flops | bytes accessed | tf_op | source)
XLA Modules:
  0.0 268.1 jit_solution(1985289216560657253)
XLA Ops:
  7.8 6.8 %collective-permute-done = bf16[128,128]{1,0:T(8,128)(2,1)S(1)} collective-permute-done((bf16[128,128]{1,0:T(8,128)(2,1)}, bf16[128,128]{1,0:T(8,128)(2,1)S(1)}, u32[]{:S(2)}, u32[]{:S(2)}) %collective-permute-start) | collective-permute-done | bytes 32800 | tf_op jit(solution)/shard_map/ppermute | solution.py:103
  14.6 6.0 %collective-permute-done.1 = bf16[128,128]{1,0:T(8,128)(2,1)S(1)} collective-permute-done((bf16[128,128]{1,0:T(8,128)(2,1)S(1)}, bf16[128,128]{1,0:T(8,128)(2,1)S(1)}, u32[]{:S(2)}, u32[]{:S(2)}) %collective-permute-start.1) | collective-permute-done | bytes 32800 | tf_op jit(solution)/shard_map/ppermute | solution.py:103
  20.6 6.0 %collective-permute-done.2 = bf16[128,128]{1,0:T(8,128)(2,1)S(1)} collective-permute-done((bf16[128,128]{1,0:T(8,128)(2,1)S(1)}, bf16[128,128]{1,0:T(8,128)(2,1)S(1)}, u32[]{:S(2)}, u32[]{:S(2)}) %collective-permute-start.2) | collective-permute-done | bytes 32800 | tf_op jit(solution)/shard_map/ppermute | solution.py:103
  26.6 6.0 %collective-permute-done.3 = bf16[128,128]{1,0:T(8,128)(2,1)S(1)} collective-permute-done((bf16[128,128]{1,0:T(8,128)(2,1)S(1)}, bf16[128,128]{1,0:T(8,128)(2,1)S(1)}, u32[]{:S(2)}, u32[]{:S(2)}) %collective-permute-start.3) | collective-permute-done | bytes 32800 | tf_op jit(solution)/shard_map/ppermute | solution.py:103
  32.7 6.0 %collective-permute-done.4 = bf16[128,128]{1,0:T(8,128)(2,1)S(1)} collective-permute-done((bf16[128,128]{1,0:T(8,128)(2,1)S(1)}, bf16[128,128]{1,0:T(8,128)(2,1)S(1)}, u32[]{:S(2)}, u32[]{:S(2)}) %collective-permute-start.4) | collective-permute-done | bytes 32800 | tf_op jit(solution)/shard_map/ppermute | solution.py:103
  38.7 6.0 %collective-permute-done.5 = bf16[128,128]{1,0:T(8,128)(2,1)S(1)} collective-permute-done((bf16[128,128]{1,0:T(8,128)(2,1)S(1)}, bf16[128,128]{1,0:T(8,128)(2,1)S(1)}, u32[]{:S(2)}, u32[]{:S(2)}) %collective-permute-start.5) | collective-permute-done | bytes 32800 | tf_op jit(solution)/shard_map/ppermute | solution.py:103
  44.7 6.0 %collective-permute-done.6 = bf16[128,128]{1,0:T(8,128)(2,1)S(1)} collective-permute-done((bf16[128,128]{1,0:T(8,128)(2,1)S(1)}, bf16[128,128]{1,0:T(8,128)(2,1)S(1)}, u32[]{:S(2)}, u32[]{:S(2)}) %collective-permute-start.6) | collective-permute-done | bytes 32800 | tf_op jit(solution)/shard_map/ppermute | solution.py:103
  50.8 6.0 %collective-permute-done.7 = bf16[128,128]{1,0:T(8,128)(2,1)S(1)} collective-permute-done((bf16[128,128]{1,0:T(8,128)(2,1)S(1)}, bf16[128,128]{1,0:T(8,128)(2,1)S(1)}, u32[]{:S(2)}, u32[]{:S(2)}) %collective-permute-start.7) | collective-permute-done | bytes 32800 | tf_op jit(solution)/shard_map/ppermute | solution.py:103
  56.8 6.0 %collective-permute-done.8 = bf16[128,128]{1,0:T(8,128)(2,1)S(1)} collective-permute-done((bf16[128,128]{1,0:T(8,128)(2,1)S(1)}, bf16[128,128]{1,0:T(8,128)(2,1)S(1)}, u32[]{:S(2)}, u32[]{:S(2)}) %collective-permute-start.8) | collective-permute-done | bytes 32800 | tf_op jit(solution)/shard_map/ppermute | solution.py:103
  62.9 6.0 %collective-permute-done.9 = bf16[128,128]{1,0:T(8,128)(2,1)S(1)} collective-permute-done((bf16[128,128]{1,0:T(8,128)(2,1)S(1)}, bf16[128,128]{1,0:T(8,128)(2,1)S(1)}, u32[]{:S(2)}, u32[]{:S(2)}) %collective-permute-start.9) | collective-permute-done | bytes 32800 | tf_op jit(solution)/shard_map/ppermute | solution.py:103
  68.9 6.0 %collective-permute-done.10 = bf16[128,128]{1,0:T(8,128)(2,1)S(1)} collective-permute-done((bf16[128,128]{1,0:T(8,128)(2,1)S(1)}, bf16[128,128]{1,0:T(8,128)(2,1)S(1)}, u32[]{:S(2)}, u32[]{:S(2)}) %collective-permute-start.10) | collective-permute-done | bytes 32800 | tf_op jit(solution)/shard_map/ppermute | solution.py:103
  74.9 6.0 %collective-permute-done.11 = bf16[128,128]{1,0:T(8,128)(2,1)S(1)} collective-permute-done((bf16[128,128]{1,0:T(8,128)(2,1)S(1)}, bf16[128,128]{1,0:T(8,128)(2,1)S(1)}, u32[]{:S(2)}, u32[]{:S(2)}) %collective-permute-start.11) | collective-permute-done | bytes 32800 | tf_op jit(solution)/shard_map/ppermute | solution.py:103
  81.8 4.7 %all_gather.62 = bf16[256,128]{1,0:T(8,128)(2,1)} all-gather(bf16[128,128]{1,0:T(8,128)(2,1)S(1)} %convert_element_type.28), channel_id=1, replica_groups=mesh['pa'=16,'pb'=2] {'pb'}, dimensions={0}, use_global_device_ids=true | all-gather | bytes 98304 | tf_op jit(solution)/shard_map/all_gather | solution.py:113
  88.0 5.1 %collective-permute-done.13 = bf16[128,128]{1,0:T(8,128)(2,1)S(1)} collective-permute-done((bf16[128,128]{1,0:T(8,128)(2,1)S(1)}, bf16[128,128]{1,0:T(8,128)(2,1)S(1)}, u32[]{:S(2)}, u32[]{:S(2)}) %collective-permute-start.13) | collective-permute-done | bytes 32800 | tf_op jit(solution)/shard_map/ppermute | solution.py:103
  94.0 4.4 %all-gather.9 = f32[2,1,128]{2,1,0:T(1,128)S(1)} all-gather(f32[1,1,128]{2,1,0:T(1,128)} %bitcast.124), channel_id=1, replica_groups=mesh['pa'=16,'pb'=2] {'pb'}, dimensions={0}, use_global_device_ids=true | all-gather | bytes 1536 | tf_op jit(solution)/shard_map/all_gather | solution.py:109
  98.4 17.3 %all-gather.6 = f32[16,1,128]{2,1,0:T(1,128)S(1)} all-gather(f32[1,1,128]{2,1,0:T(1,128)} %bitcast.107), channel_id=1, replica_groups=mesh['pa'=16,'pb'=2] {'pa'}, dimensions={0}, use_global_device_ids=true | all-gather | bytes 8704 | tf_op jit(solution)/shard_map/all_gather | solution.py:125
  127.8 19.0 %all-gather.10 = f32[16,1,256]{2,1,0:T(1,128)S(1)} all-gather(f32[1,1,256]{2,1,0:T(1,128)S(1)} %bitcast.113), channel_id=1, replica_groups=mesh['pa'=16,'pb'=2] {'pa'}, dimensions={0}, use_global_device_ids=true | all-gather | bytes 17408 | tf_op jit(solution)/shard_map/all_gather | solution.py:135
  148.7 11.5 %while.113 = (s32[]{:T(128)}, f32[128]{0:T(128)S(1)}, f32[128]{0:T(128)S(1)}, f32[4096]{0:T(1024)S(1)}, f32[128]{0:T(128)S(1)}, /*index=5*/f32[4096]{0:T(1024)S(...) while((s32[]{:T(128)}, f32[128]{0:T(128)S(1)}, ...), condition=%wide.region_11.12_spmd.clone, body=%wide.region_8.11_spmd.clone.sunk | while | flops 17236612 | bytes 707770 | solution.py:41
  160.2 17.5 %all-gather.11 = f32[16,1,128]{2,1,0:T(1,128)S(1)} all-gather(f32[1,1,128]{2,1,0:T(1,128)S(1)} %add_bitcast_fusion.1), channel_id=1, replica_groups=mesh['pa'=16,'pb'=2] {'pa'}, dimensions={0}, use_global_device_ids=true | all-gather | bytes 8704 | tf_op jit(solution)/shard_map/all_gather | solution.py:125
  180.1 4.2 %all-gather.12 = f32[2,1,256]{2,1,0:T(1,128)S(1)} all-gather(f32[1,1,256]{2,1,0:T(1,128)S(1)} %bitcast.97), channel_id=4, replica_groups=mesh['pa'=16,'pb'=2] {'pb'}, dimensions={0}, use_global_device_ids=true | all-gather | bytes 3072 | tf_op jit(solution)/shard_map/all_gather | solution.py:14
  188.6 18.8 %all-gather.14 = f32[16,1,256]{2,1,0:T(1,128)S(1)} all-gather(f32[1,1,256]{2,1,0:T(1,128)S(1)} %bitcast.112), channel_id=1, replica_groups=mesh['pa'=16,'pb'=2] {'pa'}, dimensions={0}, use_global_device_ids=true | all-gather | bytes 17408 | tf_op jit(solution)/shard_map/all_gather | solution.py:135
  207.4 11.5 %while.115 = (s32[]{:T(128)}, f32[128]{0:T(128)S(1)}, f32[128]{0:T(128)S(1)}, f32[4096]{0:T(1024)S(1)}, f32[128]{0:T(128)S(1)}, /*index=5*/f32[4096]{0:T(1024)S(...) while((s32[]{:T(128)}, f32[128]{0:T(128)S(1)}, ...), condition=%wide.region_19.20_spmd.clone, body=%wide.region_16.19_spmd.clone.sunk | while | flops 17236612 | bytes 707770 | solution.py:41
  219.4 17.4 %all-gather.15 = f32[16,1,128]{2,1,0:T(1,128)S(1)} all-gather(f32[1,1,128]{2,1,0:T(1,128)S(1)} %get-tuple-element.1165), channel_id=1, replica_groups=mesh['pa'=16,'pb'=2] {'pa'}, dimensions={0}, use_global_device_ids=true | all-gather | bytes 8704 | tf_op jit(solution)/shard_map/all_gather | solution.py:144
  251.5 8.4 %reduce-scatter.2.cloned.1.call-done = bf16[128,128]{1,0:T(8,128)(2,1)} async-done(((bf16[256,128]{1,0:T(8,128)(2,1)}), bf16[128,128]{1,0:T(8,128)(2,1)}) %reduce-scatter.2.cloned.1.call-update) | async-done | bytes 32784 | tf_op jit(solution)/shard_map/reduce_scatter | solution.py:147
  (309 shorter events, 72.3 us)
Async XLA Ops:
  7.2 108.8 %copy-start.1 = (bf16[128,128]{1,0:T(8,128)(2,1)S(1)}, bf16[128,128]{1,0:T(8,128)(2,1)}, u32[]{:S(2)}) copy-start(bf16[128,128]{1,0:T(8,128)(2,1)} %param.17) | copy-start | bytes 98308
  7.2 139.6 %all-gather.20.cloned.1.call-start = ((), (), s32[]{:S(2)}) async-start(), calls=%async_computation.1 | async-start | bytes 1114112 | tf_op jit(solution)/shard_map/all_gather | solution.py:116
  7.2 7.3 %collective-permute-start = (bf16[128,128]{1,0:T(8,128)(2,1)}, bf16[128,128]{1,0:T(8,128)(2,1)S(1)}, u32[]{:S(2)}, u32[]{:S(2)}) collective-permute-start(bf16[128,128]{1,0:T(8,128)(2,1)} %param.17), channel_id=1, source_target_pairs={{0,2},{2,4},{4,6},{6,8},{8,10},{10,12},{12,14},{14,16},{16,18},{18... | collective-permute-start | bytes 98312 | tf_op jit(solution)/shard_map/ppermute | solution.py:103
  14.6 6.0 %collective-permute-start.1 = (bf16[128,128]{1,0:T(8,128)(2,1)S(1)}, bf16[128,128]{1,0:T(8,128)(2,1)S(1)}, u32[]{:S(2)}, u32[]{:S(2)}) collective-permute-start(bf16[128,128]{1,0:T(8,128)(2,1)S(1)} %collective-permute-done), channel_id=1, source_target_pairs={{0,2},{2,4},{4,6},{6,8},{8,10},{10,12},{12,14},{14,16},{16,18},{18... | collective-permute-start | bytes 98312 | tf_op jit(solution)/shard_map/ppermute | solution.py:103
  20.6 6.0 %collective-permute-start.2 = (bf16[128,128]{1,0:T(8,128)(2,1)S(1)}, bf16[128,128]{1,0:T(8,128)(2,1)S(1)}, u32[]{:S(2)}, u32[]{:S(2)}) collective-permute-start(bf16[128,128]{1,0:T(8,128)(2,1)S(1)} %collective-permute-done.1), channel_id=1, source_target_pairs={{0,2},{2,4},{4,6},{6,8},{8,10},{10,12},{12,14},{14,16},{16,18},{18... | collective-permute-start | bytes 98312 | tf_op jit(solution)/shard_map/ppermute | solution.py:103
  26.6 6.0 %collective-permute-start.3 = (bf16[128,128]{1,0:T(8,128)(2,1)S(1)}, bf16[128,128]{1,0:T(8,128)(2,1)S(1)}, u32[]{:S(2)}, u32[]{:S(2)}) collective-permute-start(bf16[128,128]{1,0:T(8,128)(2,1)S(1)} %collective-permute-done.2), channel_id=1, source_target_pairs={{0,2},{2,4},{4,6},{6,8},{8,10},{10,12},{12,14},{14,16},{16,18},{18... | collective-permute-start | bytes 98312 | tf_op jit(solution)/shard_map/ppermute | solution.py:103
  32.7 6.0 %collective-permute-start.4 = (bf16[128,128]{1,0:T(8,128)(2,1)S(1)}, bf16[128,128]{1,0:T(8,128)(2,1)S(1)}, u32[]{:S(2)}, u32[]{:S(2)}) collective-permute-start(bf16[128,128]{1,0:T(8,128)(2,1)S(1)} %collective-permute-done.3), channel_id=1, source_target_pairs={{0,2},{2,4},{4,6},{6,8},{8,10},{10,12},{12,14},{14,16},{16,18},{18... | collective-permute-start | bytes 98312 | tf_op jit(solution)/shard_map/ppermute | solution.py:103
  38.7 6.0 %collective-permute-start.5 = (bf16[128,128]{1,0:T(8,128)(2,1)S(1)}, bf16[128,128]{1,0:T(8,128)(2,1)S(1)}, u32[]{:S(2)}, u32[]{:S(2)}) collective-permute-start(bf16[128,128]{1,0:T(8,128)(2,1)S(1)} %collective-permute-done.4), channel_id=1, source_target_pairs={{0,2},{2,4},{4,6},{6,8},{8,10},{10,12},{12,14},{14,16},{16,18},{18... | collective-permute-start | bytes 98312 | tf_op jit(solution)/shard_map/ppermute | solution.py:103
  44.7 6.0 %collective-permute-start.6 = (bf16[128,128]{1,0:T(8,128)(2,1)S(1)}, bf16[128,128]{1,0:T(8,128)(2,1)S(1)}, u32[]{:S(2)}, u32[]{:S(2)}) collective-permute-start(bf16[128,128]{1,0:T(8,128)(2,1)S(1)} %collective-permute-done.5), channel_id=1, source_target_pairs={{0,2},{2,4},{4,6},{6,8},{8,10},{10,12},{12,14},{14,16},{16,18},{18... | collective-permute-start | bytes 98312 | tf_op jit(solution)/shard_map/ppermute | solution.py:103
  50.8 6.0 %collective-permute-start.7 = (bf16[128,128]{1,0:T(8,128)(2,1)S(1)}, bf16[128,128]{1,0:T(8,128)(2,1)S(1)}, u32[]{:S(2)}, u32[]{:S(2)}) collective-permute-start(bf16[128,128]{1,0:T(8,128)(2,1)S(1)} %collective-permute-done.6), channel_id=1, source_target_pairs={{0,2},{2,4},{4,6},{6,8},{8,10},{10,12},{12,14},{14,16},{16,18},{18... | collective-permute-start | bytes 98312 | tf_op jit(solution)/shard_map/ppermute | solution.py:103
  56.8 6.0 %collective-permute-start.8 = (bf16[128,128]{1,0:T(8,128)(2,1)S(1)}, bf16[128,128]{1,0:T(8,128)(2,1)S(1)}, u32[]{:S(2)}, u32[]{:S(2)}) collective-permute-start(bf16[128,128]{1,0:T(8,128)(2,1)S(1)} %collective-permute-done.7), channel_id=1, source_target_pairs={{0,2},{2,4},{4,6},{6,8},{8,10},{10,12},{12,14},{14,16},{16,18},{18... | collective-permute-start | bytes 98312 | tf_op jit(solution)/shard_map/ppermute | solution.py:103
  62.9 6.0 %collective-permute-start.9 = (bf16[128,128]{1,0:T(8,128)(2,1)S(1)}, bf16[128,128]{1,0:T(8,128)(2,1)S(1)}, u32[]{:S(2)}, u32[]{:S(2)}) collective-permute-start(bf16[128,128]{1,0:T(8,128)(2,1)S(1)} %collective-permute-done.8), channel_id=1, source_target_pairs={{0,2},{2,4},{4,6},{6,8},{8,10},{10,12},{12,14},{14,16},{16,18},{18... | collective-permute-start | bytes 98312 | tf_op jit(solution)/shard_map/ppermute | solution.py:103
  68.9 6.0 %collective-permute-start.10 = (bf16[128,128]{1,0:T(8,128)(2,1)S(1)}, bf16[128,128]{1,0:T(8,128)(2,1)S(1)}, u32[]{:S(2)}, u32[]{:S(2)}) collective-permute-start(bf16[128,128]{1,0:T(8,128)(2,1)S(1)} %collective-permute-done.9), channel_id=1, source_target_pairs={{0,2},{2,4},{4,6},{6,8},{8,10},{10,12},{12,14},{14,16},{16,18},{18... | collective-permute-start | bytes 98312 | tf_op jit(solution)/shard_map/ppermute | solution.py:103
  74.9 6.0 %collective-permute-start.11 = (bf16[128,128]{1,0:T(8,128)(2,1)S(1)}, bf16[128,128]{1,0:T(8,128)(2,1)S(1)}, u32[]{:S(2)}, u32[]{:S(2)}) collective-permute-start(bf16[128,128]{1,0:T(8,128)(2,1)S(1)} %collective-permute-done.10), channel_id=1, source_target_pairs={{0,2},{2,4},{4,6},{6,8},{8,10},{10,12},{12,14},{14,16},{16,18},{18... | collective-permute-start | bytes 98312 | tf_op jit(solution)/shard_map/ppermute | solution.py:103
  81.0 6.0 %collective-permute-start.12 = (bf16[128,128]{1,0:T(8,128)(2,1)S(1)}, bf16[128,128]{1,0:T(8,128)(2,1)S(1)}, u32[]{:S(2)}, u32[]{:S(2)}) collective-permute-start(bf16[128,128]{1,0:T(8,128)(2,1)S(1)} %collective-permute-done.11), channel_id=1, source_target_pairs={{0,2},{2,4},{4,6},{6,8},{8,10},{10,12},{12,14},{14,16},{16,18},{18... | collective-permute-start | bytes 98312 | tf_op jit(solution)/shard_map/ppermute | solution.py:103
  86.5 173.3 %reduce-scatter.2.cloned.1.call-start = ((), (), s32[]{:S(2)}) async-start(), calls=%async_computation.2 | async-start | bytes 98304 | tf_op jit(solution)/shard_map/reduce_scatter | solution.py:147
  87.0 6.0 %collective-permute-start.13 = (bf16[128,128]{1,0:T(8,128)(2,1)S(1)}, bf16[128,128]{1,0:T(8,128)(2,1)S(1)}, u32[]{:S(2)}, u32[]{:S(2)}) collective-permute-start(bf16[128,128]{1,0:T(8,128)(2,1)S(1)} %collective-permute-done.12), channel_id=1, source_target_pairs={{0,2},{2,4},{4,6},{6,8},{8,10},{10,12},{12,14},{14,16},{16,18},{18... | collective-permute-start | bytes 98312 | tf_op jit(solution)/shard_map/ppermute | solution.py:103
  93.0 22.7 %collective-permute-start.14 = (bf16[128,128]{1,0:T(8,128)(2,1)S(1)}, bf16[128,128]{1,0:T(8,128)(2,1)S(1)}, u32[]{:S(2)}, u32[]{:S(2)}) collective-permute-start(bf16[128,128]{1,0:T(8,128)(2,1)S(1)} %collective-permute-done.13), channel_id=1, source_target_pairs={{0,2},{2,4},{4,6},{6,8},{8,10},{10,12},{12,14},{14,16},{16,18},{18... | collective-permute-start | bytes 98312 | tf_op jit(solution)/shard_map/ppermute | solution.py:103
  116.0 0.8 copy-start
  148.6 11.6 %copy-start.3 = (f32[128]{0:T(128)S(1)}, f32[128]{0:T(128)}, u32[]{:S(2)}) copy-start(f32[128]{0:T(128)} %param.19) | copy-start | bytes 1540
  247.8 12.1 %copy-start.2 = (f32[128,128]{1,0:T(8,128)S(1)}, f32[128,128]{1,0:T(8,128)}, u32[]{:S(2)}) copy-start(f32[128,128]{1,0:T(8,128)} %param.16) | copy-start | bytes 196612
Sparse Core Ops, SparseCore 0:
  86.6 38.2 all-gather.19
  251.0 8.8 reduce-scatter.1
